TPU v7x, 32 devices: a whole 2x2x4 slice. The times are simulated.
32 devices in a mesh: row: 8 (over z, x), col: 4 (over y, core).
Axes of the slice: x: 2, y: 2, z: 4, core: 2. Of those that a mesh axis runs over, the one named last changes fastest.
Arguments:
- eigvecs: bfloat16 [49152, 4096], P('row', 'col'), may hold values from -41 to 41
- reflectors: bfloat16 [8, 49152, 128], P(None, 'row'), as said below
- factors: float32 [8, 128, 128], replicated, as said below
Outputs:
- vectors: bfloat16 [49152, 4096], P('row', 'col')
- deviation: float32 [4096], P('col')
Inputs may be any that keep to these rules, and one draw needn't show every extreme that they name: `reflectors`: each panel's vectors are dense and linearly independent. factors[k] is the upper triangular compact WY factor of reflectors[k]: its inverse plus its inverse's transpose equals reflectors[k]^T reflectors[k], so that I - reflectors[k] factors[k] reflectors[k]^T is orthogonal up to rounding.
All inputs are finite; a program needn't handle non-finite values.
Results may differ from a plain program's by a relative error of at most 0.014.
Values may be sent and summed in bfloat16 or wider, within the bound.
A program may use at most 128 MiB of HBM per device.

v0:
```python
import jax
import jax.numpy as jnp
from jax import lax
from jax.sharding import PartitionSpec as P

NORD = 49152


def body(eigvecs, reflectors, factors):
    vectors = eigvecs
    panels = reflectors.shape[0]
    width = reflectors.shape[2]
    local_rows = reflectors.shape[1]
    stacked = jnp.transpose(reflectors, (1, 0, 2)).reshape(local_rows, panels * width)
    local_proj = lax.dot_general(
        stacked, eigvecs, (((0,), (0,)), ((), ())), preferred_element_type=jnp.float32
    )
    local_gram = lax.dot_general(
        stacked, stacked, (((0,), (0,)), ((), ())), preferred_element_type=jnp.float32
    )
    total_proj, total_gram = (
        lax.psum(local_proj.astype(jnp.bfloat16), "row").astype(jnp.float32),
        lax.psum(local_gram.astype(jnp.bfloat16), "row").astype(jnp.float32),
    )
    earlier = []
    for panel in range(panels):
        proj = total_proj[panel * width : (panel + 1) * width]
        for prior in range(panel):
            cross = total_gram[
                panel * width : (panel + 1) * width, prior * width : (prior + 1) * width
            ]
            proj = proj - jnp.dot(
                cross, earlier[prior].astype(jnp.float32), precision=lax.Precision.HIGHEST
            )
        scaled = jnp.dot(factors[panel], proj, precision=lax.Precision.HIGHEST).astype(jnp.bfloat16)
        earlier.append(scaled)
        update = jnp.dot(reflectors[panel], scaled, preferred_element_type=jnp.float32)
        vectors = (vectors.astype(jnp.float32) - update).astype(jnp.bfloat16)
    wide = vectors.astype(jnp.float32)
    local_squares = jnp.sum(wide * wide, axis=0)
    squares = lax.psum(local_squares, "row")
    deviation = jnp.sqrt(squares / NORD) - 1.0
    return (vectors, deviation)


def solution(mesh):
    placed = (P("row", "col"), P(None, "row", None), P())
    return jax.shard_map(
        body, mesh=mesh, in_specs=placed, out_specs=(P("row", "col"), P("col")), check_vma=False
    )
```

profile of v0, /device:TPU:0, one launch (start us, length us, event | category | flops | bytes accessed | tf_op | source)
XLA Modules:
  0.0 387.1 jit_solution(8457546555832240318)
XLA Ops:
  7.2 0.0 all-reduce.3.cloned.1.call-start
  7.2 16.6 %copy.8 = bf16[8,6144,128]{1,2,0:T(8,128)(2,1)} copy(bf16[8,6144,128]{2,1,0:T(8,128)(2,1)} %param.4) | data formatting | bytes 25165824 | tf_op args[1]
  23.8 0.0 copy-start
  23.8 19.0 %convolution_convert_fusion = bf16[1024,1024]{1,0:T(8,128)(2,1)} fusion(bf16[6144,1024]{0,1:T(8,128)(2,1)} %bitcast.132), kind=kOutput, calls=%fused_computation.17 | convolution fusion | flops 12885950464 | bytes 14680064 | tf_op jit(solution)/shard_map/dot_general | solution.py:18
  42.8 0.0 copy-done
  42.8 16.9 %convolution_convert_fusion.1 = bf16[1024,1024]{1,0:T(8,128)(2,1)} fusion(bf16[6144,1024]{0,1:T(8,128)(2,1)} %bitcast.133, bf16[6144,1024]{1,0:T(8,128)(2,1)S(1)} %copy-done), kind=kOutput, calls=%fused_computation.18 | convolution fusion | flops 12885950464 | bytes 27262976 | tf_op jit(solution)/shard_map/dot_general | solution.py:15
  59.7 0.0 all-reduce.3.cloned.1.call-update
  59.7 16.2 %copy.7 = bf16[6144,1024]{0,1:T(8,128)(2,1)} copy(bf16[6144,1024]{1,0:T(8,128)(2,1)} %param.3) | data formatting | bytes 25165824 | tf_op args[0]
  75.9 143.1 %all-reduce.3.cloned.1.call-done = (bf16[1024,1024]{1,0:T(8,128)(2,1)}, bf16[1024,1024]{1,0:T(8,128)(2,1)}) async-done(((bf16[1024,1024]{1,0:T(8,128)(2,1)}, bf16[1024,1024]{1,0:T(8,128)(2,1)}), (bf16[1024,1024]{1,0:T(8,128)(2,1)}, bf16[1024,1024]{1,0:T(8,128)(2,1)})) %all-reduce.3.cloned.1.call-update) | async-done | bytes 4194320 | tf_op jit(solution)/shard_map/psum | solution.py:22
  219.0 2.0 convert_element_type.126
  221.1 1.4 convolution_convert_fusion.9
  222.5 1.0 convolution_subtract_fusion.27
  223.5 1.8 convolution_subtract_fusion.26
  225.2 1.0 convolution_subtract_fusion.24
  226.2 1.0 convolution_subtract_fusion.21
  227.2 1.0 convolution_subtract_fusion.17
  228.2 1.0 convolution_subtract_fusion.12
  229.2 1.0 convolution_subtract_fusion.6
  230.2 1.8 convolution_convert_fusion.8
  232.1 9.8 %fusion.7 = bf16[6144,1024]{0,1:T(8,128)(2,1)} fusion(bf16[6144,1024]{0,1:T(8,128)(2,1)} %copy.7, bf16[1024,128]{1,0:T(8,128)(2,1)S(1)} %convolution_convert_fusion.9, bf16[8,6144,128]{2,1,0:T(8,128)(2,1)} %param.4), kind=kOutput, calls=%fused_computation.15 | convolution fusion | flops 1629487104 | bytes 27000832 | tf_op jit(solution)/shard_map/dot_general | solution.py:37
  241.9 9.8 %fusion.6 = bf16[6144,1024]{0,1:T(8,128)(2,1)} fusion(bf16[6144,1024]{0,1:T(8,128)(2,1)} %fusion.7, bf16[1024,128]{1,0:T(8,128)(2,1)S(1)} %convolution_convert_fusion.8, bf16[8,6144,128]{2,1,0:T(8,128)(2,1)} %param.4), kind=kOutput, calls=%fused_computation.13 | convolution fusion | flops 1629487104 | bytes 27000832 | tf_op jit(solution)/shard_map/dot_general | solution.py:37
  251.7 1.3 convolution_subtract_fusion.25
  253.0 1.8 convolution_convert_fusion.7
  254.8 1.8 convolution_subtract_fusion.23
  256.6 0.0 copy-start.1
  256.6 9.9 %fusion.5 = bf16[6144,1024]{0,1:T(8,128)(2,1)} fusion(bf16[6144,1024]{0,1:T(8,128)(2,1)} %fusion.6, bf16[1024,128]{1,0:T(8,128)(2,1)S(1)} %convolution_convert_fusion.7, bf16[8,6144,128]{2,1,0:T(8,128)(2,1)} %param.4), kind=kOutput, calls=%fused_computation.11 | convolution fusion | flops 1629487104 | bytes 27000832 | tf_op jit(solution)/shard_map/dot_general | solution.py:37
  266.5 0.0 copy-done.1
  266.5 1.0 convolution_subtract_fusion.22
  267.4 1.8 convolution_convert_fusion.6
  269.3 1.0 convolution_subtract_fusion.20
  270.3 1.0 convolution_subtract_fusion.19
  271.3 9.8 %fusion.4 = bf16[6144,1024]{0,1:T(8,128)(2,1)} fusion(bf16[6144,1024]{0,1:T(8,128)(2,1)} %fusion.5, bf16[1024,128]{1,0:T(8,128)(2,1)S(1)} %convolution_convert_fusion.6, bf16[8,6144,128]{2,1,0:T(8,128)(2,1)} %param.4), kind=kOutput, calls=%fused_computation.9 | convolution fusion | flops 1629487104 | bytes 27000832 | tf_op jit(solution)/shard_map/dot_general | solution.py:37
  281.1 1.0 convolution_subtract_fusion.18
  282.1 1.8 convolution_convert_fusion.5
  283.9 1.0 convolution_subtract_fusion.16
  284.9 1.0 convolution_subtract_fusion.15
  285.9 1.0 convolution_subtract_fusion.14
  286.9 9.8 %fusion.3 = bf16[6144,1024]{0,1:T(8,128)(2,1)} fusion(bf16[6144,1024]{0,1:T(8,128)(2,1)} %fusion.4, bf16[1024,128]{1,0:T(8,128)(2,1)S(1)} %convolution_convert_fusion.5, bf16[8,6144,128]{2,1,0:T(8,128)(2,1)} %param.4), kind=kOutput, calls=%fused_computation.7 | convolution fusion | flops 1629487104 | bytes 27000832 | tf_op jit(solution)/shard_map/dot_general | solution.py:37
  296.7 1.0 convolution_subtract_fusion.13
  297.7 1.8 convolution_convert_fusion.4
  299.6 1.0 convolution_subtract_fusion.11
  300.6 1.0 convolution_subtract_fusion.10
  301.5 1.0 convolution_subtract_fusion.9
  302.5 1.0 convolution_subtract_fusion.8
  303.5 9.8 %fusion.2 = bf16[6144,1024]{0,1:T(8,128)(2,1)} fusion(bf16[6144,1024]{0,1:T(8,128)(2,1)} %fusion.3, bf16[1024,128]{1,0:T(8,128)(2,1)S(1)} %convolution_convert_fusion.4, bf16[8,6144,128]{2,1,0:T(8,128)(2,1)} %param.4), kind=kOutput, calls=%fused_computation.5 | convolution fusion | flops 1629487104 | bytes 27000832 | tf_op jit(solution)/shard_map/dot_general | solution.py:37
  313.3 1.0 convolution_subtract_fusion.7
  314.3 1.8 convolution_convert_fusion.3
  316.2 1.0 convolution_subtract_fusion.5
  317.2 1.0 convolution_subtract_fusion.4
  318.2 1.0 convolution_subtract_fusion.3
  319.2 1.0 convolution_subtract_fusion.2
  320.2 1.0 convolution_subtract_fusion.1
  321.1 9.8 %fusion.1 = bf16[6144,1024]{0,1:T(8,128)(2,1)} fusion(bf16[6144,1024]{0,1:T(8,128)(2,1)} %fusion.2, bf16[1024,128]{1,0:T(8,128)(2,1)S(1)} %convolution_convert_fusion.3, bf16[8,6144,128]{2,1,0:T(8,128)(2,1)} %param.4), kind=kOutput, calls=%fused_computation.3 | convolution fusion | flops 1629487104 | bytes 27000832 | tf_op jit(solution)/shard_map/dot_general | solution.py:37
  331.0 1.0 convolution_subtract_fusion
  332.0 1.8 convolution_convert_fusion.2
  333.8 10.1 %multiply_reduce_fusion = (f32[1024]{0:T(1024)S(1)}, bf16[6144,1024]{0,1:T(8,128)(2,1)}) fusion(bf16[1024,128]{1,0:T(8,128)(2,1)S(1)} %convolution_convert_fusion.2, bf16[8,6144,128]{2,1,0:T(8,128)(2,1)} %param.4, bf16[6144,1024]{0,1:T(8,128)(2,1)} %fusion.1), kind=kOutput, calls=%fused_computation.16 | convolution fusion | flops 1648360448 | bytes 27004928 | tf_op jit(solution)/shard_map/dot_general | solution.py:37
  343.9 16.6 %copy.9 = bf16[6144,1024]{1,0:T(8,128)(2,1)} copy(bf16[6144,1024]{0,1:T(8,128)(2,1)} %get-tuple-element.9) | data formatting | bytes 25165824
  360.5 19.1 %psum.23 = f32[1024]{0:T(1024)S(1)} all-reduce(f32[1024]{0:T(1024)S(1)} %get-tuple-element.8), channel_id=1, replica_groups=mesh['row'=8,'col'=4] {'row'}, use_global_device_ids=true, to_apply=%region_3.0 | all-reduce | flops 1024 | bytes 8192 | tf_op jit(solution)/shard_map/psum | solution.py:41
  379.6 0.6 sqrt_add_fusion
Async XLA Ops:
  7.2 211.8 %all-reduce.3.cloned.1.call-start = ((), (), s32[]{:S(2)}) async-start(), calls=%async_computation | async-start | bytes 8388608 | tf_op jit(solution)/shard_map/psum | solution.py:22
  23.8 19.0 %copy-start = (bf16[6144,1024]{1,0:T(8,128)(2,1)S(1)}, bf16[6144,1024]{1,0:T(8,128)(2,1)}, u32[]{:S(2)}) copy-start(bf16[6144,1024]{1,0:T(8,128)(2,1)} %param.3) | copy-start | bytes 37748740
  256.6 9.9 %copy-start.1 = (f32[128,1024]{1,0:T(8,128)S(1)}, f32[128,1024]{1,0:T(8,128)}, u32[]{:S(2)}) copy-start(f32[128,1024]{1,0:T(8,128)} %convolution_subtract_fusion.23) | copy-start | bytes 1572868
Sparse Core Ops, SparseCore 0:
  59.9 159.1 all-reduce.2
where the time goes:
time: 391 us; the launch traced here: 387 us
  matrix products  158 us (40%)
  waiting for transfers between devices  143 us (37%)
  local copies, waits for them, and re-layouts  49.4 us (13%)
  blocking collectives  19.1 us (5%)
  between operations  14.3 us (4%)
    psum x1, waiting for transfers between devices, body(): lax.psum(local_proj.astype(jnp.bfloat16), 'row').astype(jnp.float32)  143 us
    dot_general x8, matrix products, body(): jnp.dot(reflectors[panel], scaled, preferred_element_type=jnp.float32)  78.9 us
    unnamed x7, local copies, waits for them, and re-layouts  49.4 us
    dot_general x28, matrix products, body(): jnp.dot(cross, earlier[prior].astype(jnp.float32), precision=lax.Precisio...  29.5 us
    psum x1, blocking collectives, body(): squares = lax.psum(local_squares, 'row')  19.1 us
    dot_general x1, matrix products, body(): lax.dot_general(stacked, stacked, (((0,), (0,)), ((), ())), preferred_ele...  19 us
    dot_general x1, matrix products, body(): lax.dot_general(stacked, eigvecs, (((0,), (0,)), ((), ())), preferred_ele...  16.9 us
    dot_general x8, matrix products, body(): jnp.dot(factors[panel], proj, precision=lax.Precision.HIGHEST)  14.3 us
  transfers between devices with their start and end apart: 1, of which 1 were waited for; matrix products, arithmetic and copies ran while one was open for 4% of the time, Pallas kernels for 0%

commit v1 on v0

--- a/solution.py
+++ b/solution.py
@@ -4,6 +4,12 @@
 from jax.sharding import PartitionSpec as P
 
 NORD = 49152
+
+
+def gather_and_add(x, mesh_axis):
+    parts = lax.all_gather(x, mesh_axis, axis=0, tiled=False)
+    acc = parts.sum(axis=0)
+    return acc
 
 
 def body(eigvecs, reflectors, factors):
@@ -19,7 +25,7 @@
         stacked, stacked, (((0,), (0,)), ((), ())), preferred_element_type=jnp.float32
     )
     total_proj, total_gram = (
-        lax.psum(local_proj.astype(jnp.bfloat16), "row").astype(jnp.float32),
+        gather_and_add(local_proj.astype(jnp.bfloat16), "row").astype(jnp.float32),
         lax.psum(local_gram.astype(jnp.bfloat16), "row").astype(jnp.float32),
     )
     earlier = []

time: 391 us -> 539 us (1.38)
  waiting for transfers between devices: 143 us -> 286 us
  other arithmetic: 2.64 us -> 12.7 us
    all_gather x0 -> x1, waiting for transfers between devices: none -> 194 us  [gather_and_add(): parts = lax.all_gather(x, mesh_axis, axis=0, tiled=False)]
    psum x1, waiting for transfers between devices: 143 us -> 91.6 us  [body(): lax.psum(local_gram.astype(jnp.bfloat16), 'row').astype(jnp.float32)]
    reduce_sum x0 -> x1, other arithmetic: none -> 9.67 us  [gather_and_add(): acc = parts.sum(axis=0)]
    dot_general x8, matrix products: 14.3 us -> 7.41 us  [body(): jnp.dot(factors[panel], proj, precision=lax.Precision.HIGHEST)]
    unnamed x7 -> x5, local copies, waits for them, and re-layouts: 49.4 us -> 49.8 us
  transfers between devices with their start and end apart: 1 -> 2, of which waited for: 1 -> 2; matrix products, arithmetic and copies ran while one was open for 4% -> 9% of each run, Pallas kernels for 0% -> 0%
where the time goes in v1:
time: 539 us; the launch traced here: 536 us
  waiting for transfers between devices  286 us (53%)
  matrix products  153 us (28%)
  local copies, waits for them, and re-layouts  49.8 us (9%)
  blocking collectives  19.6 us (4%)
  between operations  14.3 us (3%)
  other arithmetic  12.7 us (2%)
    all_gather x1, waiting for transfers between devices, gather_and_add(): parts = lax.all_gather(x, mesh_axis, axis=0, tiled=False)  194 us
    psum x1, waiting for transfers between devices, body(): lax.psum(local_gram.astype(jnp.bfloat16), 'row').astype(jnp.float32)  91.6 us
    dot_general x8, matrix products, body(): jnp.dot(reflectors[panel], scaled, preferred_element_type=jnp.float32)  78.8 us
    unnamed x5, local copies, waits for them, and re-layouts  49.8 us
    dot_general x28, matrix products, body(): jnp.dot(cross, earlier[prior].astype(jnp.float32), precision=lax.Precisio...  29.7 us
    psum x1, blocking collectives, body(): squares = lax.psum(local_squares, 'row')  19.6 us
    dot_general x1, matrix products, body(): lax.dot_general(stacked, stacked, (((0,), (0,)), ((), ())), preferred_ele...  18.8 us
    dot_general x1, matrix products, body(): lax.dot_general(stacked, eigvecs, (((0,), (0,)), ((), ())), preferred_ele...  18.7 us
  transfers between devices with their start and end apart: 2, of which 2 were waited for; matrix products, arithmetic and copies ran while one was open for 9% of the time, Pallas kernels for 0%

profile of v1, /device:TPU:0, one launch (start us, length us, event | category | flops | bytes accessed | tf_op | source)
XLA Modules:
  0.0 536.3 jit_solution(6553943589801509986)
XLA Ops:
  7.2 0.0 all-gather.3.cloned.1.call-start
  7.2 16.6 %copy.8 = bf16[8,6144,128]{1,2,0:T(8,128)(2,1)} copy(bf16[8,6144,128]{2,1,0:T(8,128)(2,1)} %param.4) | data formatting | bytes 25165824 | tf_op args[1]
  23.8 18.7 %convolution_convert_fusion.1 = bf16[1024,1024]{1,0:T(8,128)(2,1)} fusion(bf16[6144,1024]{0,1:T(8,128)(2,1)} %bitcast.134, bf16[6144,1024]{1,0:T(8,128)(2,1)} %param.3), kind=kOutput, calls=%fused_computation.18 | convolution fusion | flops 12885950464 | bytes 27262976 | tf_op jit(solution)/shard_map/dot_general | solution.py:21
  42.5 0.0 all-gather.3.cloned.1.call-update
  42.5 0.2 all-reduce.2.cloned.1.call-start
  42.8 18.8 %convolution_convert_fusion = bf16[1024,1024]{1,0:T(8,128)(2,1)} fusion(bf16[6144,1024]{0,1:T(8,128)(2,1)} %bitcast.135), kind=kOutput, calls=%fused_computation.17 | convolution fusion | flops 12885950464 | bytes 14680064 | tf_op jit(solution)/shard_map/dot_general | solution.py:24
  61.6 0.0 all-reduce.2.cloned.1.call-update
  61.6 16.6 %copy.7 = bf16[6144,1024]{0,1:T(8,128)(2,1)} copy(bf16[6144,1024]{1,0:T(8,128)(2,1)} %param.3) | data formatting | bytes 25165824 | tf_op args[0]
  78.2 194.5 %all-gather.3.cloned.1.call-done = bf16[8192,1024]{1,0:T(8,128)(2,1)} async-done(((bf16[1024,1024]{1,0:T(8,128)(2,1)}), bf16[8192,1024]{1,0:T(8,128)(2,1)}) %all-gather.3.cloned.1.call-update) | async-done | bytes 16777232 | tf_op jit(solution)/shard_map/all_gather | solution.py:10
  272.7 9.7 %reduce_sum.21 = bf16[1024,1024]{1,0:T(8,128)(2,1)S(1)} reduce(bf16[8,1024,1024]{2,1,0:T(8,128)(2,1)} %bitcast.133, bf16[]{:T(256)} %constant.6.clone.1), dimensions={0}, to_apply=%region_0.0 | reduce | flops 7340032 | bytes 18874370 | tf_op jit(solution)/shard_map/reduce_sum | solution.py:11
  282.4 0.0 copy-start
  282.4 2.4 convert_element_type.128
  284.8 0.0 copy-done
  284.8 0.4 convolution_convert_fusion.9
  285.2 91.6 %all-reduce.2.cloned.1.call-done = bf16[1024,1024]{1,0:T(8,128)(2,1)} async-done(((bf16[1024,1024]{1,0:T(8,128)(2,1)}), bf16[1024,1024]{1,0:T(8,128)(2,1)}) %all-reduce.2.cloned.1.call-update) | async-done | bytes 2097168 | tf_op jit(solution)/shard_map/psum | solution.py:29
  376.8 1.3 convolution_subtract_fusion.27
  378.1 1.0 convolution_convert_fusion.8
  379.1 1.3 convolution_subtract_fusion.26
  380.4 1.0 convolution_subtract_fusion.25
  381.4 1.0 convolution_convert_fusion.7
  382.4 9.8 %fusion.7 = bf16[6144,1024]{0,1:T(8,128)(2,1)} fusion(bf16[6144,1024]{0,1:T(8,128)(2,1)} %copy.7, bf16[1024,128]{1,0:T(8,128)(2,1)S(1)} %convolution_convert_fusion.9, bf16[8,6144,128]{2,1,0:T(8,128)(2,1)} %param.4), kind=kOutput, calls=%fused_computation.15 | convolution fusion | flops 1629487104 | bytes 27000832 | tf_op jit(solution)/shard_map/dot_general | solution.py:43
  392.3 9.8 %fusion.6 = bf16[6144,1024]{0,1:T(8,128)(2,1)} fusion(bf16[6144,1024]{0,1:T(8,128)(2,1)} %fusion.7, bf16[1024,128]{1,0:T(8,128)(2,1)S(1)} %convolution_convert_fusion.8, bf16[8,6144,128]{2,1,0:T(8,128)(2,1)} %param.4), kind=kOutput, calls=%fused_computation.13 | convolution fusion | flops 1629487104 | bytes 27000832 | tf_op jit(solution)/shard_map/dot_general | solution.py:43
  402.1 9.8 %fusion.5 = bf16[6144,1024]{0,1:T(8,128)(2,1)} fusion(bf16[6144,1024]{0,1:T(8,128)(2,1)} %fusion.6, bf16[1024,128]{1,0:T(8,128)(2,1)S(1)} %convolution_convert_fusion.7, bf16[8,6144,128]{2,1,0:T(8,128)(2,1)} %param.4), kind=kOutput, calls=%fused_computation.11 | convolution fusion | flops 1629487104 | bytes 27000832 | tf_op jit(solution)/shard_map/dot_general | solution.py:43
  411.9 1.3 convolution_subtract_fusion.24
  413.2 1.0 convolution_subtract_fusion.23
  414.2 1.0 convolution_subtract_fusion.22
  415.1 1.0 convolution_convert_fusion.6
  416.1 9.8 %fusion.4 = bf16[6144,1024]{0,1:T(8,128)(2,1)} fusion(bf16[6144,1024]{0,1:T(8,128)(2,1)} %fusion.5, bf16[1024,128]{1,0:T(8,128)(2,1)S(1)} %convolution_convert_fusion.6, bf16[8,6144,128]{2,1,0:T(8,128)(2,1)} %param.4), kind=kOutput, calls=%fused_computation.9 | convolution fusion | flops 1629487104 | bytes 27000832 | tf_op jit(solution)/shard_map/dot_general | solution.py:43
  426.0 1.3 convolution_subtract_fusion.21
  427.3 1.0 convolution_subtract_fusion.20
  428.3 1.0 convolution_subtract_fusion.19
  429.3 1.0 convolution_subtract_fusion.18
  430.2 1.0 convolution_convert_fusion.5
  431.2 9.8 %fusion.3 = bf16[6144,1024]{0,1:T(8,128)(2,1)} fusion(bf16[6144,1024]{0,1:T(8,128)(2,1)} %fusion.4, bf16[1024,128]{1,0:T(8,128)(2,1)S(1)} %convolution_convert_fusion.5, bf16[8,6144,128]{2,1,0:T(8,128)(2,1)} %param.4), kind=kOutput, calls=%fused_computation.7 | convolution fusion | flops 1629487104 | bytes 27000832 | tf_op jit(solution)/shard_map/dot_general | solution.py:43
  441.1 1.3 convolution_subtract_fusion.17
  442.4 1.0 convolution_subtract_fusion.16
  443.4 1.0 convolution_subtract_fusion.15
  444.3 1.0 convolution_subtract_fusion.14
  445.3 1.0 convolution_subtract_fusion.13
  446.3 1.0 convolution_convert_fusion.4
  447.3 9.8 %fusion.2 = bf16[6144,1024]{0,1:T(8,128)(2,1)} fusion(bf16[6144,1024]{0,1:T(8,128)(2,1)} %fusion.3, bf16[1024,128]{1,0:T(8,128)(2,1)S(1)} %convolution_convert_fusion.4, bf16[8,6144,128]{2,1,0:T(8,128)(2,1)} %param.4), kind=kOutput, calls=%fused_computation.5 | convolution fusion | flops 1629487104 | bytes 27000832 | tf_op jit(solution)/shard_map/dot_general | solution.py:43
  457.2 1.3 convolution_subtract_fusion.12
  458.5 1.0 convolution_subtract_fusion.11
  459.4 1.0 convolution_subtract_fusion.10
  460.4 1.0 convolution_subtract_fusion.9
  461.4 1.0 convolution_subtract_fusion.8
  462.4 1.0 convolution_subtract_fusion.7
  463.4 1.0 convolution_convert_fusion.3
  464.4 9.8 %fusion.1 = bf16[6144,1024]{0,1:T(8,128)(2,1)} fusion(bf16[6144,1024]{0,1:T(8,128)(2,1)} %fusion.2, bf16[1024,128]{1,0:T(8,128)(2,1)S(1)} %convolution_convert_fusion.3, bf16[8,6144,128]{2,1,0:T(8,128)(2,1)} %param.4), kind=kOutput, calls=%fused_computation.3 | convolution fusion | flops 1629487104 | bytes 27000832 | tf_op jit(solution)/shard_map/dot_general | solution.py:43
  474.2 1.3 convolution_subtract_fusion.6
  475.5 1.0 convolution_subtract_fusion.5
  476.5 1.0 convolution_subtract_fusion.4
  477.5 1.0 convolution_subtract_fusion.3
  478.5 1.0 convolution_subtract_fusion.2
  479.5 1.0 convolution_subtract_fusion.1
  480.5 1.0 convolution_subtract_fusion
  481.5 1.0 convolution_convert_fusion.2
  482.5 10.1 %multiply_reduce_fusion = (f32[1024]{0:T(1024)S(1)}, bf16[6144,1024]{0,1:T(8,128)(2,1)}) fusion(bf16[1024,128]{1,0:T(8,128)(2,1)S(1)} %convolution_convert_fusion.2, bf16[8,6144,128]{2,1,0:T(8,128)(2,1)} %param.4, bf16[6144,1024]{0,1:T(8,128)(2,1)} %fusion.1), kind=kOutput, calls=%fused_computation.16 | convolution fusion | flops 1648360448 | bytes 27004928 | tf_op jit(solution)/shard_map/dot_general | solution.py:43
  492.7 16.6 %copy.9 = bf16[6144,1024]{1,0:T(8,128)(2,1)} copy(bf16[6144,1024]{0,1:T(8,128)(2,1)} %get-tuple-element.7) | data formatting | bytes 25165824
  509.2 19.6 %psum.15 = f32[1024]{0:T(1024)S(1)} all-reduce(f32[1024]{0:T(1024)S(1)} %get-tuple-element.6), channel_id=1, replica_groups=mesh['row'=8,'col'=4] {'row'}, use_global_device_ids=true, to_apply=%region_3.0 | all-reduce | flops 1024 | bytes 8192 | tf_op jit(solution)/shard_map/psum | solution.py:47
  528.8 0.6 sqrt_add_fusion
Async XLA Ops:
  7.2 265.5 %all-gather.3.cloned.1.call-start = ((), (), s32[]{:S(2)}) async-start(), calls=%async_computation.1 | async-start | bytes 18874368 | tf_op jit(solution)/shard_map/all_gather | solution.py:10
  42.5 334.3 %all-reduce.2.cloned.1.call-start = ((), (), s32[]{:S(2)}) async-start(), calls=%async_computation | async-start | bytes 4194304 | tf_op jit(solution)/shard_map/psum | solution.py:29
  282.4 2.4 copy-start
Sparse Core Ops, SparseCore 0:
  42.7 229.9 all-gather.2
  276.3 100.4 all-reduce.1
